TPU v7x, 32 devices: a whole 2x2x4 slice. The times are simulated.
32 devices in a mesh: lat: 4 (over z), lon: 8 (over y, x, core).
Axes of the slice: x: 2, y: 2, z: 4, core: 2. Of those that a mesh axis runs over, the one named last changes fastest.
Arguments:
- observations: bfloat16 [49152, 128], P(('lat', 'lon')), may hold values from -6 to 6
- owner_device: int32 [49152, 1], P(('lat', 'lon')), may hold values from 0 to 31; in each aligned block of 1536 rows (0 to 1535, 1536 to 3071, ...) at most 96 rows name the same one
- local_cell: int32 [49152], P(('lat', 'lon')), may hold values from 0 to 383
- valid_counts: int32 [32], P(('lat', 'lon')), may hold values from 768 to 1536
- weight_in: bfloat16 [128, 256], replicated, may hold values from -0.5 to 0.5
- bias_in: float32 [256], replicated, may hold values from -3 to 3
- weight_out: bfloat16 [256, 256], replicated, may hold values from -0.375 to 0.375
- kernel_taps: float32 [9, 256], replicated, may hold values from -2 to 2
- cotangent: bfloat16 [64, 192, 256], P(('lat', 'lon')), may hold values from -6 to 6
Outputs:
- grid_out: bfloat16 [64, 192, 256], P(('lat', 'lon'))
- grad_weight_in: float32 [128, 256], replicated
- grad_bias_in: float32 [256], replicated
- grad_weight_out: float32 [256, 256], replicated
- grad_kernel: float32 [9, 256], replicated
Inputs may be any that keep to these rules, and one draw needn't show every extreme that they name: `owner_device`: within the rows of one block, at most 96 rows name one owner, and in every draw some block names some owner exactly 96 times.
All inputs are finite; a program needn't handle non-finite values.
Results may differ from a plain program's by a relative error of at most 0.0065.
Values may be sent and summed in bfloat16 or wider, within the bound.
A program may use at most 64 MiB of HBM per device.

v0:
```python
import math

import jax
import jax.numpy as jnp
from jax import lax
from jax.sharding import PartitionSpec as P

OFFSETS = [(shift_lat, shift_lon) for shift_lat in (-1, 0, 1) for shift_lon in (-1, 0, 1)]


def extended(shard, sides, width):
    for axis, dim in sides:
        count, length = (lax.axis_size(axis), shard.shape[dim])
        up = [(i, (i + 1) % count) for i in range(count)]
        down = [(j, i) for i, j in up]
        last = lax.slice_in_dim(shard, length - width, length, axis=dim)
        first = lax.slice_in_dim(shard, 0, width, axis=dim)
        before = lax.ppermute(last, axis, up)
        after = lax.ppermute(first, axis, down)
        shard = jnp.concatenate([before, shard, after], axis=dim)
    return shard


def encoder(rows, weight_in, bias_in, weight_out):
    before = jnp.dot(rows, weight_in, preferred_element_type=jnp.float32) + bias_in
    hidden = jax.nn.gelu(before).astype(jnp.bfloat16)
    encoded = jnp.dot(hidden, weight_out, preferred_element_type=jnp.float32).astype(jnp.bfloat16)
    return (before, hidden, encoded)


def local_grads(rows, before, hidden, upstream, weight_out):
    contract = (((0,), (0,)), ((), ()))
    grad_out = lax.dot_general(hidden, upstream, contract, preferred_element_type=jnp.float32)
    back = lax.dot_general(
        upstream, weight_out, (((1,), (1,)), ((), ())), preferred_element_type=jnp.float32
    )
    _, pullback = jax.vjp(jax.nn.gelu, before)
    pre_grad = pullback(back)[0].astype(jnp.bfloat16)
    grad_in = lax.dot_general(rows, pre_grad, contract, preferred_element_type=jnp.float32)
    grad_bias = jnp.sum(pre_grad.astype(jnp.float32), axis=0)
    return (grad_in, grad_bias, grad_out)


def edge_mask(padded, tile_rows):
    lat_count = lax.axis_size("lat")
    lat_here = lax.axis_index("lat")
    row_ids = jnp.arange(tile_rows + 2, dtype=jnp.int32)
    outside = (row_ids == 0) & (lat_here == 0) | (row_ids == tile_rows + 1) & (
        lat_here == lat_count - 1
    )
    keep_rows = jnp.logical_not(outside).astype(padded.dtype)
    return padded * keep_rows[:, None, None]


def local(
    observations,
    owner_device,
    local_cell,
    valid_counts,
    weight_in,
    bias_in,
    weight_out,
    kernel_taps,
    cotangent,
):
    lat_count = lax.axis_size("lat")
    lon_count = lax.axis_size("lon")
    devices_all = lat_count * lon_count
    obs_rows = observations.shape[0]
    channels = weight_out.shape[1]
    capacity = 2 * obs_rows // devices_all
    tile_rows = cotangent.shape[0] * lon_count
    tile_cols = cotangent.shape[1] // lon_count
    cells_tile = tile_rows * tile_cols
    owners = owner_device[:, 0]
    valid_rows = jnp.arange(obs_rows, dtype=jnp.int32) < valid_counts[0]
    matches = (owners[:, None] == jnp.arange(devices_all, dtype=jnp.int32)[None, :]).astype(
        jnp.int32
    )
    earlier = jnp.sum((jnp.cumsum(matches, axis=0) - 1) * matches, axis=1)
    slot_index = owners * capacity + earlier
    sent_cells = jnp.full((devices_all * capacity,), cells_tile, jnp.int32)
    sent_cells = sent_cells.at[slot_index].set(jnp.where(valid_rows, local_cell, cells_tile))
    got_cells = lax.all_to_all(
        sent_cells.reshape(devices_all, capacity),
        ("lat", "lon"),
        split_axis=0,
        concat_axis=0,
        tiled=True,
    ).reshape(-1)
    width = observations.shape[1]
    outgoing = (
        jnp.zeros((devices_all * capacity, width), observations.dtype)
        .at[slot_index]
        .set(observations)
    )
    arrived = lax.all_to_all(
        outgoing.reshape(devices_all, capacity, width),
        ("lat", "lon"),
        split_axis=0,
        concat_axis=0,
        tiled=True,
    )
    arrived_rows = arrived.reshape(devices_all * capacity, width)
    before, hidden, arrived_enc = encoder(arrived_rows, weight_in, bias_in, weight_out)
    deposit = jax.ops.segment_sum(
        arrived_enc.astype(jnp.float32), got_cells, num_segments=cells_tile + 1
    )
    deposit = deposit[:cells_tile].reshape(tile_rows, tile_cols, channels)
    padded = extended(deposit, (("lat", 0), ("lon", 1)), 1)
    padded = edge_mask(padded, tile_rows)
    grid_field = jnp.zeros((tile_rows, tile_cols, channels), jnp.float32)
    for tap_index, (shift_lat, shift_lon) in enumerate(OFFSETS):
        window = padded[
            1 + shift_lat : 1 + shift_lat + tile_rows, 1 + shift_lon : 1 + shift_lon + tile_cols
        ]
        grid_field = grid_field + kernel_taps[tap_index] * window
    grid_out = lax.all_to_all(
        grid_field.astype(jnp.bfloat16), "lon", split_axis=0, concat_axis=1, tiled=True
    )
    loss_scale = 1.0 / math.sqrt(obs_rows * devices_all)
    cot_tile = lax.all_to_all(cotangent, "lon", split_axis=1, concat_axis=0, tiled=True)
    cot_float = cot_tile.astype(jnp.float32)
    cot_padded = extended(cot_tile, (("lat", 0), ("lon", 1)), 1)
    cot_padded = edge_mask(cot_padded, tile_rows).astype(jnp.float32)
    kernel_rows = []
    adjoint = jnp.zeros((tile_rows, tile_cols, channels), jnp.float32)
    for tap_index, (shift_lat, shift_lon) in enumerate(OFFSETS):
        window = padded[
            1 + shift_lat : 1 + shift_lat + tile_rows, 1 + shift_lon : 1 + shift_lon + tile_cols
        ]
        kernel_rows.append(loss_scale * jnp.sum(cot_float * window, axis=(0, 1)))
        back_window = cot_padded[
            1 - shift_lat : 1 - shift_lat + tile_rows, 1 - shift_lon : 1 - shift_lon + tile_cols
        ]
        adjoint = adjoint + kernel_taps[tap_index] * back_window
    grad_kernel = jnp.stack(kernel_rows)
    adjoint = (loss_scale * adjoint).astype(jnp.bfloat16)
    adjoint_rows = jnp.concatenate(
        [adjoint.reshape(cells_tile, channels), jnp.zeros((1, channels), jnp.bfloat16)], axis=0
    )
    upstream = adjoint_rows[got_cells]
    grads = local_grads(arrived_rows, before, hidden, upstream, weight_out)
    grad_in, grad_bias, grad_out, grad_kernel = lax.psum(
        (grads[0], grads[1], grads[2], grad_kernel), ("lat", "lon")
    )
    return (grid_out, grad_in, grad_bias, grad_out, grad_kernel)


def solution(mesh):
    return jax.shard_map(
        local,
        mesh=mesh,
        in_specs=(
            P(("lat", "lon"), None),
            P(("lat", "lon"), None),
            P(("lat", "lon")),
            P(("lat", "lon")),
            P(),
            P(),
            P(),
            P(),
            P(("lat", "lon"), None, None),
        ),
        out_specs=(P(("lat", "lon"), None, None), P(), P(), P(), P()),
        check_vma=False,
    )
```

profile of v0, /device:TPU:0, one launch (start us, length us, event | category | flops | bytes accessed | tf_op | source)
XLA Modules:
  0.0 270.5 jit_solution(18164300997538134326)
XLA Ops:
  8.6 9.1 %reduce-window.6 = s32[32,12,128]{2,1,0:T(8,128)S(1)} reduce-window(s32[32,12,128]{2,1,0:T(8,128)S(1)} %fusion.30, s32[]{:T(128)} %constant.21.clone.1), window={size=1x1x128 pad=0_0x0_0x127_0}, to_apply=%region_0.0 | reduce-window | flops 6242304 | bytes 393220 | tf_op jit(solution)/shard_map/reduce-window
  19.8 6.2 %scatter_custom_fusion = s32[3072]{0:T(1024)S(1)} fusion(s32[1536]{0:T(1024)S(1)} %fusion.36, s32[1536]{0:T(1024)S(1)} %fusion.35, s32[]{:T(128)} %constant.19.clone.1), kind=kCustom, calls=%fused_computation.84 | custom fusion | bytes 12292 | tf_op jit(solution)/shard_map/scatter | solution.py:83
  26.7 7.3 %all-to-all-start = ((s32[32,1,96]{2,1,0:T(1,128)}), s32[32,1,96]{2,1,0:T(1,128)S(1)}, u32[]{:S(2)}, u32[]{:S(2)}) async-start(s32[32,1,96]{2,1,0:T(1,128)} %all_to_all.35), calls=%async_computation | async-start | bytes 32768 | tf_op jit(solution)/shard_map/all_to_all | solution.py:84
  34.1 1.8 copy.23
  35.9 5.7 %scatter_custom_fusion.1 = bf16[3072,128]{1,0:T(8,128)(2,1)} fusion(s32[1536]{0:T(1024)S(1)} %fusion.36, bf16[1536,128]{1,0:T(8,128)(2,1)} %param.9, bf16[]{:T(256)} %constant.24.clone.1), kind=kCustom, calls=%fused_computation.57 | custom fusion | bytes 786944 | tf_op jit(solution)/shard_map/scatter | solution.py:95
  41.6 3.9 %all-to-all-start.3 = ((bf16[2,192,256]{2,0,1:T(2,128)(2,1)}), bf16[2,192,256]{2,0,1:T(2,128)(2,1)S(1)}, u32[]{:S(2)}, u32[]{:S(2)}) async-start(bf16[2,192,256]{2,0,1:T(2,128)(2,1)} %copy.23), calls=%async_computation.3 | async-start | bytes 393216 | tf_op jit(solution)/shard_map/all_to_all | solution.py:122
  45.7 6.1 %all-to-all-done.3 = bf16[2,192,256]{2,0,1:T(2,128)(2,1)S(1)} async-done(((bf16[2,192,256]{2,0,1:T(2,128)(2,1)}), bf16[2,192,256]{2,0,1:T(2,128)(2,1)S(1)}, u32[]{:S(2)}, u32[]{:S(2)}) %all-to-all-start.3) | async-done | bytes 196640 | tf_op jit(solution)/shard_map/all_to_all | solution.py:122
  51.8 3.7 %all-to-all-start.1 = ((bf16[32,96,128]{2,1,0:T(8,128)(2,1)}), bf16[32,96,128]{2,1,0:T(8,128)(2,1)S(1)}, u32[]{:S(2)}, u32[]{:S(2)}) async-start(bf16[32,96,128]{2,1,0:T(8,128)(2,1)} %bitcast.4), calls=%async_computation.1 | async-start | bytes 1572864 | tf_op jit(solution)/shard_map/all_to_all | solution.py:97
  55.6 1.8 collective-permute-start.4
  57.4 2.1 collective-permute-start.5
  59.5 13.7 %collective-permute-done.4 = bf16[1,24,256]{2,1,0:T(8,128)(2,1)S(1)} collective-permute-done((bf16[1,24,256]{2,1,0:T(8,128)(2,1)S(1)}, bf16[1,24,256]{2,1,0:T(8,128)(2,1)S(1)}, u32[]{:S(2)}, u32[]{:S(2)}) %collective-permute-start.4) | collective-permute-done | bytes 12320 | tf_op jit(solution)/shard_map/ppermute | solution.py:18
  73.3 2.6 collective-permute-start.7
  77.9 11.1 %gather_fusion = bf16[3072,256]{1,0:T(8,128)(2,1)S(1)} fusion(bf16[385,256]{1,0:T(8,128)(2,1)S(1)} %concatenate.19, s32[3072]{0:T(1024)S(1)} %broadcast_clamp_fusion), kind=kCustom, calls=%fused_computation | custom fusion | bytes 3158016 | tf_op jit(solution)/shard_map/gather | solution.py:142
  89.0 2.3 fusion.45
  91.3 5.0 %convert_reduce_fusion = (f32[256]{0:T(256)S(1)}, bf16[3072,256]{1,0:T(8,128)(2,1)}, f32[3072,256]{1,0:T(8,128)S(1)}) fusion(f32[3072,256]{1,0:T(8,128)} %fusion.45, f32[256]{0:T(256)S(1)} %copy-done.4, bf16[3072,128]{1,0:T(8,128)(2,1)S(1)} %bitcast.78, bf16[128,256]{1,0:T(8,128)(2,1)S(1)} %copy-done.3), kind=kOutput, calls=%fused_computation.16 | convolution fusion | flops 219414272 | bytes 8718336 | tf_op jit(solution)/shard_map/dot_general | solution.py:25
  97.9 2.8 %fusion = f32[3072,256]{1,0:T(8,128)} fusion(bf16[256,256]{1,0:T(8,128)(2,1)S(1)} %copy-done, f32[3072,256]{1,0:T(8,128)S(1)} %get-tuple-element.37), kind=kOutput, calls=%fused_computation.8 | convolution fusion | flops 411303936 | bytes 6422528 | tf_op jit(solution)/shard_map/dot_general | solution.py:27
  100.7 19.4 %scatter_custom_fusion.2 = f32[385,256]{1,0:T(8,128)S(1)} fusion(s32[3072]{0:T(1024)S(1)} %reshape.214, f32[3072,256]{1,0:T(8,128)} %fusion, f32[]{:T(128)} %constant.18.clone.1), kind=kCustom, calls=%fused_computation.64 | custom fusion | flops 786432 | bytes 394752 | tf_op jit(solution)/shard_map/scatter-add | solution.py:106
  120.1 4.9 %collective-permute-start = (f32[1,24,256]{2,1,0:T(8,128)S(1)}, f32[1,24,256]{2,1,0:T(8,128)S(1)}, u32[]{:S(2)}, u32[]{:S(2)}) collective-permute-start(f32[1,24,256]{2,1,0:T(8,128)S(1)} %get-tuple-element.22), channel_id=1, source_target_pairs={{0,8},{8,16},{16,24},{24,0},{1,9},{9,17},{17,25},{25,1},{2,10},{10... | collective-permute-start | bytes 73736 | tf_op jit(solution)/shard_map/ppermute | solution.py:18
  125.0 3.9 %fusion.41 = f32[256,256]{1,0:T(8,128)} fusion(bf16[3072,256]{1,0:T(8,128)(2,1)S(1)} %gather_fusion, f32[3072,256]{1,0:T(8,128)} %copy-done.5), kind=kOutput, calls=%fused_computation.98 | convolution fusion | flops 409731072 | bytes 4980736 | tf_op jit(solution)/shard_map/dot_general | solution.py:33
  129.1 2.8 %collective-permute-start.3 = (f32[18,1,256]{2,1,0:T(1,128)S(1)}, f32[18,1,256]{2,1,0:T(1,128)S(1)}, u32[]{:S(2)}, u32[]{:S(2)}) collective-permute-start(f32[18,1,256]{2,1,0:T(1,128)S(1)} %get-tuple-element.21), channel_id=1, source_target_pairs={{1,0},{2,1},{3,2},{4,3},{5,4},{6,5},{7,6},{0,7},{9,8},{10,9},{11,1... | collective-permute-start | bytes 55304 | tf_op jit(solution)/shard_map/ppermute | solution.py:19
  134.8 3.9 %all-to-all-start.2 = ((bf16[16,24,256]{2,1,0:T(8,128)(2,1)}), bf16[16,24,256]{2,1,0:T(8,128)(2,1)S(1)}, u32[]{:S(2)}, u32[]{:S(2)}) async-start(bf16[16,24,256]{2,1,0:T(8,128)(2,1)} %add_convert_fusion), calls=%async_computation.2 | async-start | bytes 393216 | tf_op jit(solution)/shard_map/all_to_all | solution.py:118
  138.8 41.3 %all-reduce.1 = (f32[256]{0:T(256)}, f32[9,256]{1,0:T(8,128)}) all-reduce(f32[256]{0:T(256)S(1)} %get-tuple-element.18, f32[9,256]{1,0:T(8,128)S(1)} %stack.2), channel_id=1, replica_groups=mesh['lat'=4,'lon'=8] {'lat','lon'}, use_global_device_ids=true, to_apply=%region_8.9 | all-reduce | flops 2560 | bytes 20480 | tf_op jit(solution)/shard_map/psum | solution.py:144
  180.8 79.7 %all-reduce.5.cloned.1.call-done = (f32[128,256]{1,0:T(8,128)}, f32[256,256]{1,0:T(8,128)}) async-done(((f32[128,256]{1,0:T(8,128)}, f32[256,256]{1,0:T(8,128)}), (f32[128,256]{1,0:T(8,128)}, f32[256,256]{1,0:T(8,128)})) %all-reduce.5.cloned.1.call-update) | async-done | bytes 393232 | tf_op jit(solution)/shard_map/psum | solution.py:144
  262.0 1.7 copy.31
  (68 shorter events, 12.7 us)
Async XLA Ops:
  7.2 81.8 %copy-start = (bf16[256,256]{1,0:T(8,128)(2,1)S(1)}, bf16[256,256]{1,0:T(8,128)(2,1)}, u32[]{:S(2)}) copy-start(bf16[256,256]{1,0:T(8,128)(2,1)} %param.15) | copy-start | bytes 393220
  7.2 38.4 %copy-start.2 = (f32[9,256]{1,0:T(8,128)S(1)}, f32[9,256]{1,0:T(8,128)}, u32[]{:S(2)}) copy-start(f32[9,256]{1,0:T(8,128)} %param.16) | copy-start | bytes 27652
  26.7 14.9 %all-to-all-start = ((s32[32,1,96]{2,1,0:T(1,128)}), s32[32,1,96]{2,1,0:T(1,128)S(1)}, u32[]{:S(2)}, u32[]{:S(2)}) async-start(s32[32,1,96]{2,1,0:T(1,128)} %all_to_all.35), calls=%async_computation | async-start | bytes 32768 | tf_op jit(solution)/shard_map/all_to_all | solution.py:84
  41.6 10.1 %all-to-all-start.3 = ((bf16[2,192,256]{2,0,1:T(2,128)(2,1)}), bf16[2,192,256]{2,0,1:T(2,128)(2,1)S(1)}, u32[]{:S(2)}, u32[]{:S(2)}) async-start(bf16[2,192,256]{2,0,1:T(2,128)(2,1)} %copy.23), calls=%async_computation.3 | async-start | bytes 393216 | tf_op jit(solution)/shard_map/all_to_all | solution.py:122
  51.8 39.5 %all-to-all-start.1 = ((bf16[32,96,128]{2,1,0:T(8,128)(2,1)}), bf16[32,96,128]{2,1,0:T(8,128)(2,1)S(1)}, u32[]{:S(2)}, u32[]{:S(2)}) async-start(bf16[32,96,128]{2,1,0:T(8,128)(2,1)} %bitcast.4), calls=%async_computation.1 | async-start | bytes 1572864 | tf_op jit(solution)/shard_map/all_to_all | solution.py:97
  55.5 204.9 %all-reduce.5.cloned.1.call-start = ((), (), s32[]{:S(2)}) async-start(), calls=%async_computation.4 | async-start | bytes 786432 | tf_op jit(solution)/shard_map/psum | solution.py:144
  55.6 17.6 %collective-permute-start.4 = (bf16[1,24,256]{2,1,0:T(8,128)(2,1)S(1)}, bf16[1,24,256]{2,1,0:T(8,128)(2,1)S(1)}, u32[]{:S(2)}, u32[]{:S(2)}) collective-permute-start(bf16[1,24,256]{2,1,0:T(8,128)(2,1)S(1)} %get-tuple-element.26), channel_id=1, source_target_pairs={{0,8},{8,16},{16,24},{24,0},{1,9},{9,17},{17,25},{25,1},{2,10},{10... | collective-permute-start | bytes 36872 | tf_op jit(solution)/shard_map/ppermute | solution.py:18
  57.4 15.8 %collective-permute-start.5 = (bf16[1,24,256]{2,1,0:T(8,128)(2,1)S(1)}, bf16[1,24,256]{2,1,0:T(8,128)(2,1)S(1)}, u32[]{:S(2)}, u32[]{:S(2)}) collective-permute-start(bf16[1,24,256]{2,1,0:T(8,128)(2,1)S(1)} %get-tuple-element.27), channel_id=1, source_target_pairs={{8,0},{16,8},{24,16},{0,24},{9,1},{17,9},{25,17},{1,25},{10,2},{18... | collective-permute-start | bytes 36872 | tf_op jit(solution)/shard_map/ppermute | solution.py:19
  73.3 4.1 %collective-permute-start.6 = (bf16[18,1,256]{2,1,0:T(2,128)(2,1)S(1)}, bf16[18,1,256]{2,1,0:T(2,128)(2,1)S(1)}, u32[]{:S(2)}, u32[]{:S(2)}) collective-permute-start(bf16[18,1,256]{2,1,0:T(2,128)(2,1)S(1)} %get-tuple-element.24), channel_id=1, source_target_pairs={{0,1},{1,2},{2,3},{3,4},{4,5},{5,6},{6,7},{7,0},{8,9},{9,10},{10,1... | collective-permute-start | bytes 27656 | tf_op jit(solution)/shard_map/ppermute | solution.py:18
  73.3 4.1 %collective-permute-start.7 = (bf16[18,1,256]{2,1,0:T(2,128)(2,1)S(1)}, bf16[18,1,256]{2,1,0:T(2,128)(2,1)S(1)}, u32[]{:S(2)}, u32[]{:S(2)}) collective-permute-start(bf16[18,1,256]{2,1,0:T(2,128)(2,1)S(1)} %get-tuple-element.25), channel_id=1, source_target_pairs={{1,0},{2,1},{3,2},{4,3},{5,4},{6,5},{7,6},{0,7},{9,8},{10,9},{11,1... | collective-permute-start | bytes 27656 | tf_op jit(solution)/shard_map/ppermute | solution.py:19
  89.0 2.3 copy-start.3
  89.0 2.3 copy-start.4
  96.2 1.7 copy-start.5
  120.1 8.9 %collective-permute-start = (f32[1,24,256]{2,1,0:T(8,128)S(1)}, f32[1,24,256]{2,1,0:T(8,128)S(1)}, u32[]{:S(2)}, u32[]{:S(2)}) collective-permute-start(f32[1,24,256]{2,1,0:T(8,128)S(1)} %get-tuple-element.22), channel_id=1, source_target_pairs={{0,8},{8,16},{16,24},{24,0},{1,9},{9,17},{17,25},{25,1},{2,10},{10... | collective-permute-start | bytes 73736 | tf_op jit(solution)/shard_map/ppermute | solution.py:18
  125.0 6.9 %copy-start.1 = (bf16[3072,256]{1,0:T(8,128)(2,1)S(1)}, bf16[3072,256]{1,0:T(8,128)(2,1)}, u32[]{:S(2)}) copy-start(bf16[3072,256]{1,0:T(8,128)(2,1)} %get-tuple-element.19) | copy-start | bytes 4718596
  125.0 3.9 %collective-permute-start.1 = (f32[1,24,256]{2,1,0:T(8,128)S(1)}, f32[1,24,256]{2,1,0:T(8,128)S(1)}, u32[]{:S(2)}, u32[]{:S(2)}) collective-permute-start(f32[1,24,256]{2,1,0:T(8,128)S(1)} %get-tuple-element.23), channel_id=1, source_target_pairs={{8,0},{16,8},{24,16},{0,24},{9,1},{17,9},{25,17},{1,25},{10,2},{18... | collective-permute-start | bytes 73736 | tf_op jit(solution)/shard_map/ppermute | solution.py:19
  129.0 4.3 %collective-permute-start.2 = (f32[18,1,256]{2,1,0:T(1,128)S(1)}, f32[18,1,256]{2,1,0:T(1,128)S(1)}, u32[]{:S(2)}, u32[]{:S(2)}) collective-permute-start(f32[18,1,256]{2,1,0:T(1,128)S(1)} %get-tuple-element.20), channel_id=1, source_target_pairs={{0,1},{1,2},{2,3},{3,4},{4,5},{5,6},{6,7},{7,0},{8,9},{9,10},{10,1... | collective-permute-start | bytes 55304 | tf_op jit(solution)/shard_map/ppermute | solution.py:18
  129.1 4.3 %collective-permute-start.3 = (f32[18,1,256]{2,1,0:T(1,128)S(1)}, f32[18,1,256]{2,1,0:T(1,128)S(1)}, u32[]{:S(2)}, u32[]{:S(2)}) collective-permute-start(f32[18,1,256]{2,1,0:T(1,128)S(1)} %get-tuple-element.21), channel_id=1, source_target_pairs={{1,0},{2,1},{3,2},{4,3},{5,4},{6,5},{7,6},{0,7},{9,8},{10,9},{11,1... | collective-permute-start | bytes 55304 | tf_op jit(solution)/shard_map/ppermute | solution.py:19
  134.8 45.3 %all-to-all-start.2 = ((bf16[16,24,256]{2,1,0:T(8,128)(2,1)}), bf16[16,24,256]{2,1,0:T(8,128)(2,1)S(1)}, u32[]{:S(2)}, u32[]{:S(2)}) async-start(bf16[16,24,256]{2,1,0:T(8,128)(2,1)} %add_convert_fusion), calls=%async_computation.2 | async-start | bytes 393216 | tf_op jit(solution)/shard_map/all_to_all | solution.py:118
Sparse Core Ops, SparseCore 0:
  133.1 127.2 all-reduce.4
where the time goes:
time: 272 us; the launch traced here: 271 us
  waiting for transfers between devices  100 us (37%)
  blocking collectives  41.3 us (15%)
  other arithmetic  33.5 us (12%)
  starting transfers between devices  33.3 us (12%)
  local copies, waits for them, and re-layouts  32.3 us (12%)
  matrix products  15 us (6%)
  between operations  15 us (6%)
    psum x1, waiting for transfers between devices, local(): lax.psum((grads[0], grads[1], grads[2], grad_kernel), ('lat', 'lon'))  79.7 us
    psum x1, blocking collectives, local(): lax.psum((grads[0], grads[1], grads[2], grad_kernel), ('lat', 'lon'))  41.3 us
    scatter-add x1, other arithmetic, local(): jax.ops.segment_sum(arrived_enc.astype(jnp.float32), got_cells, num_segme...  19.4 us
    ppermute x4, waiting for transfers between devices, extended(): before = lax.ppermute(last, axis, up)  14.2 us
    gather x1, local copies, waits for them, and re-layouts, local(): upstream = adjoint_rows[got_cells]  11.1 us
    another operation x2, other arithmetic  9.11 us
    ppermute x4, starting transfers between devices, extended(): after = lax.ppermute(first, axis, down)  7.52 us
    all_to_all x1, starting transfers between devices, local(): lax.all_to_all(sent_cells.reshape(devices_all, capacity), ('lat', 'lon'),...  7.33 us
  transfers between devices with their start and end apart: 13, of which 6 were waited for; matrix products, arithmetic and copies ran while one was open for 11% of the time, Pallas kernels for 0%

commit v1 on v0

v1 whole, which is shorter than its diff:
```python
import functools
import math

import jax
import jax.numpy as jnp
from jax import lax
from jax.experimental import pallas as pl
from jax.experimental.pallas import tpu as pltpu
from jax.sharding import PartitionSpec as P

MESH = pl.DeviceIdType.MESH
F32 = jnp.float32
BF16 = jnp.bfloat16
OFFSETS = [(a, b) for a in (-1, 0, 1) for b in (-1, 0, 1)]
CURVE = math.sqrt(2.0 / math.pi)
META = 16
GROUP = 4


def round_up(value, step):
    return -(-value // step) * step


def iota(shape, dim):
    return lax.broadcasted_iota(jnp.int32, shape, dim)


def dot(left, right, contract=((1,), (0,))):
    return lax.dot_general(left, right, (contract, ((), ())), preferred_element_type=F32)


def kernel(
    n_lat, n_lon, slots, piece, scale,
    obs, owner, cell, count, w_in, b_in, w_out, taps, cot,
    grid_o, gin_o, gb_o, gout_o, gk_o,
    meta, slot_row, sbuf, rbuf, cot_top, cot_bot, adj_s, adj_r, adj_f, adj_b,
    dep, dep_b, dep_r, hal_top, hal_bot, strip, total, parts, gathered, gk_s, gk_r,
    row_send, row_recv, cot_send, cot_recv, adj_send, adj_recv, dep_send, dep_recv,
    hal_send, hal_recv, sum_send, sum_recv, all_send, all_recv, gk_send, gk_recv,
):
    n = n_lat * n_lon
    lat, lon = lax.axis_index("lat"), lax.axis_index("lon")
    me = lat * n_lon + lon
    obs_rows, feat = obs.shape
    own_rows, cols, channels = cot.shape
    tile_rows = own_rows * n_lon
    tile_cols = cols // n_lon
    cells = tile_rows * tile_cols
    hidden_size = w_in.shape[1]
    groups = n // GROUP

    def place(target):
        return (target // n_lon, lax.rem(target, n_lon))

    def remote(src, dst, send, recv, device):
        return pltpu.make_async_remote_copy(
            src_ref=src, dst_ref=dst, send_sem=send, recv_sem=recv,
            device_id=device, device_id_type=MESH,
        )

    def drain(ref, sem):
        pltpu.make_async_copy(ref, ref, sem).wait()

    barrier = pltpu.get_barrier_semaphore()

    def greet(off, carry):
        pl.semaphore_signal(
            barrier, inc=1, device_id=place(lax.rem(me + off, n)), device_id_type=MESH
        )
        return carry

    lax.fori_loop(1, n, greet, 0)

    @pl.when(me == 0)
    def _():
        cot_top[...] = jnp.zeros_like(cot_top)

    @pl.when(me == n - 1)
    def _():
        cot_bot[...] = jnp.zeros_like(cot_bot)

    has_top = jnp.logical_and(lon == 0, lat > 0)
    has_bot = jnp.logical_and(lon == n_lon - 1, lat < n_lat - 1)

    @pl.when(jnp.logical_not(has_top))
    def _():
        hal_top[...] = jnp.zeros_like(hal_top)

    @pl.when(jnp.logical_not(has_bot))
    def _():
        hal_bot[...] = jnp.zeros_like(hal_bot)

    dep[...] = jnp.zeros_like(dep)
    total[...] = jnp.zeros_like(total)
    dep_b[0] = jnp.zeros((tile_cols, channels), BF16)
    dep_b[tile_rows + 1] = jnp.zeros((tile_cols, channels), BF16)

    own_row = owner[...]
    match = (own_row == iota((n, obs_rows), 0)).astype(F32)
    block = 256 if obs_rows % 256 == 0 else 128
    upper = (iota((block, block), 0) < iota((block, block), 1)).astype(F32).astype(BF16)
    carry = jnp.zeros((n, 1), F32)
    ranks = []
    for start in range(0, obs_rows, block):
        part = match[:, start:start + block]
        before = dot(part.astype(BF16), upper) + carry
        ranks.append(jnp.sum(before * part, axis=0, keepdims=True))
        carry = carry + jnp.sum(part, axis=1, keepdims=True)
    rank = jnp.concatenate(ranks, axis=1).astype(jnp.int32)
    slot_row[...] = own_row * slots + rank
    lane = iota((1, obs_rows), 1)
    code = jnp.where(lane < count[0], cell[...] + 1, 0)
    high = (code // 128).astype(F32)
    low = lax.rem(code, 128).astype(F32)
    coded = jnp.concatenate([match * high, match * low], axis=0).astype(BF16)
    by_rank = (rank == iota((128, obs_rows), 0)).astype(F32).astype(BF16)
    meta[...] = dot(coded, by_rank, ((1,), (1,)))

    pl.semaphore_wait(barrier, n - 1)

    up_copy = remote(cot.at[own_rows - 1], cot_top, cot_send.at[0], cot_recv.at[0], place(lax.rem(me + 1, n)))
    down_copy = remote(cot.at[0], cot_bot, cot_send.at[1], cot_recv.at[1], place(lax.rem(me + n - 1, n)))

    @pl.when(me < n - 1)
    def _():
        up_copy.start()

    @pl.when(me > 0)
    def _():
        down_copy.start()

    def row_copy(off, g):
        return remote(
            sbuf.at[off], rbuf.at[off], row_send, row_recv.at[g], place(lax.rem(me + off, n))
        )

    def send_group(g, carry, first=False):
        ids = slot_row[...]
        picks = []
        for q in range(GROUP):
            target = lax.rem(me + g * GROUP + q, n)
            pick = (ids - target * slots) == iota((slots, obs_rows), 0)
            picks.append(pick.astype(F32).astype(BF16))
        rows = dot(jnp.concatenate(picks, axis=0), obs[...]).astype(BF16)
        line = iota((META, 128), 0)
        for q in range(GROUP):
            off = g * GROUP + q
            target = lax.rem(me + off, n)
            sbuf[off, :slots, :] = rows[q * slots:(q + 1) * slots]
            tail = jnp.where(
                line == 0, meta[pl.ds(target, 1), :],
                jnp.where(line == 1, meta[pl.ds(n + target, 1), :], 0.0),
            )
            sbuf[off, slots:slots + META, :] = tail.astype(BF16)
        for q in range(GROUP):
            if first and q == 0:
                pltpu.make_async_copy(sbuf.at[0], rbuf.at[0], row_recv.at[0]).start()
            else:
                row_copy(g * GROUP + q, g).start()
        return carry

    send_group(0, 0, True)

    @pl.when(me > 0)
    def _():
        up_copy.wait_recv()

    @pl.when(me < n - 1)
    def _():
        down_copy.wait_recv()

    tap = taps[...]

    def shifts(row):
        return {0: row, 1: pltpu.roll(row, 1, 0), -1: pltpu.roll(row, cols - 1, 0)}

    cot_rows = [cot_top[...]] + [cot[r] for r in range(own_rows)] + [cot_bot[...]]
    sums = [jnp.zeros((cols, channels), F32) for _ in range(own_rows)]
    for at, row in enumerate(cot_rows):
        moved = shifts(row.astype(F32))
        for y in range(own_rows):
            a = y - (at - 1)
            if abs(a) <= 1:
                for b in (-1, 0, 1):
                    k = 3 * (a + 1) + b + 1
                    sums[y] = sums[y] + tap[k:k + 1] * moved[b]
    for y in range(own_rows):
        value = scale * sums[y]
        for j in range(n_lon):
            adj_s[j, y] = value[j * tile_cols:(j + 1) * tile_cols].astype(BF16)

    def adj_copy(step):
        other = lax.rem(lon + step, n_lon)
        return remote(
            adj_s.at[other], adj_r.at[lon], adj_send, adj_recv, (lat, other)
        )

    for step in range(1, n_lon):
        adj_copy(step).start()
    adj_r[lon] = adj_s[lon]

    lax.fori_loop(1, groups, send_group, 0)

    drain(adj_r.at[pl.ds(0, n_lon - 1)], adj_recv)
    for k in range(n_lon):
        for y in range(own_rows):
            m = k * own_rows + y
            adj_f[m * tile_cols:(m + 1) * tile_cols, :] = adj_r[k, y].astype(F32)
    adj_b[...] = adj_f[...].astype(BF16)

    bias_at = hidden_size + feat

    def take_group(g, carry):
        held = rbuf.at[pl.ds(g * GROUP, GROUP)]
        drain(held, row_recv.at[g])
        rows = jnp.concatenate([rbuf[g * GROUP + q, :slots, :] for q in range(GROUP)], axis=0)
        same = iota((slots, 128), 0) == iota((slots, 128), 1)
        spread = []
        for q in range(GROUP):
            tail = rbuf[g * GROUP + q, slots:slots + META, :].astype(F32)
            spread.append(jnp.concatenate(
                [jnp.where(same, tail[0:1], 0.0), jnp.where(same, tail[1:2], 0.0)], axis=1
            ).astype(BF16))
        weigh = jnp.where(iota((256, 128), 0) < 128, 128.0, 1.0).astype(BF16)
        codes = dot(jnp.concatenate(spread, axis=0), weigh).astype(jnp.int32)
        lanes = iota(codes.shape, 1) + 1
        pick = jnp.concatenate(
            [(codes == lanes + at).astype(F32).astype(BF16) for at in range(0, cells, 128)], axis=1
        )
        x = dot(rows, w_in[...]) + b_in[...]
        square = x * x
        t = jnp.tanh(CURVE * (x + 0.044715 * (square * x)))
        half = 0.5 * (1.0 + t)
        hidden = (x * half).astype(BF16)
        slope = half + 0.5 * x * (1.0 - t * t) * (CURVE * (1.0 + 3.0 * 0.044715 * square))
        encoded = dot(hidden, w_out[...]).astype(BF16)
        dep[...] += dot(pick, encoded, ((0,), (0,)))
        upstream = dot(pick, adj_b[...]).astype(BF16)
        back = dot(upstream, w_out[...], ((1,), (1,)))
        pre = (back * slope).astype(BF16)
        total[0:hidden_size, :] += dot(hidden, upstream, ((0,), (0,)))
        total[hidden_size:bias_at, :] += dot(rows, pre, ((0,), (0,)))
        total[bias_at:bias_at + 1, :] += jnp.sum(pre.astype(F32), axis=0, keepdims=True)
        return carry

    lax.fori_loop(0, groups, take_group, 0)

    for m in range(tile_rows):
        dep_b[m + 1] = dep[m * tile_cols:(m + 1) * tile_cols, :].astype(BF16)

    def dep_copy(step):
        other = lax.rem(lon + step, n_lon)
        return remote(
            dep_b.at[pl.ds(other * own_rows, own_rows + 2)], dep_r.at[lon],
            dep_send, dep_recv, (lat, other),
        )

    low_copy = remote(
        dep_b.at[tile_rows], hal_top.at[lon], hal_send.at[0], hal_recv.at[0],
        (lax.rem(lat + 1, n_lat), 0),
    )
    high_copy = remote(
        dep_b.at[1], hal_bot.at[lon], hal_send.at[1], hal_recv.at[1],
        (lax.rem(lat + n_lat - 1, n_lat), n_lon - 1),
    )

    @pl.when(lat < n_lat - 1)
    def _():
        low_copy.start()

    @pl.when(lat > 0)
    def _():
        high_copy.start()

    for step in range(1, n_lon):
        dep_copy(step).start()
    dep_r[lon] = dep_b[pl.ds(lon * own_rows, own_rows + 2)]

    def span(at):
        return pl.ds(pl.multiple_of(at * piece, 8), piece)

    def sum_start(off, carry):
        target = lax.rem(me + off, n)
        remote(total.at[span(target)], parts.at[off - 1], sum_send, sum_recv, place(target)).start()
        return carry

    lax.fori_loop(1, n, sum_start, 0)

    drain(dep_r.at[pl.ds(0, n_lon - 1)], dep_recv)

    @pl.when(has_top)
    def _():
        drain(hal_top, hal_recv.at[0])

    @pl.when(has_bot)
    def _():
        drain(hal_bot, hal_recv.at[1])

    for j in range(n_lon):
        for r in range(own_rows + 2):
            value = dep_r[j, r].astype(F32)
            if r == 0:
                value = value + hal_top[j].astype(F32)
            if r == own_rows + 1:
                value = value + hal_bot[j].astype(F32)
            strip[r, j * tile_cols:(j + 1) * tile_cols, :] = value

    fields = [jnp.zeros((cols, channels), F32) for _ in range(own_rows)]
    kernel_rows = [jnp.zeros((1, channels), F32) for _ in OFFSETS]
    for at in range(own_rows + 2):
        moved = shifts(strip[at])
        for y in range(own_rows):
            a = at - 1 - y
            if abs(a) <= 1:
                for b in (-1, 0, 1):
                    k = 3 * (a + 1) + b + 1
                    fields[y] = fields[y] + tap[k:k + 1] * moved[-b]
                    kernel_rows[k] = kernel_rows[k] + jnp.sum(
                        cot[y].astype(F32) * moved[-b], axis=0, keepdims=True
                    )
    for y in range(own_rows):
        grid_o[y] = fields[y].astype(BF16)
    spare = gk_s.shape[0] - len(OFFSETS)
    gk_s[...] = scale * jnp.concatenate(kernel_rows + [jnp.zeros((spare, channels), F32)], axis=0)

    def gk_start(off, carry):
        target = lax.rem(me + off, n)
        remote(gk_s, gk_r.at[off - 1], gk_send, gk_recv, place(target)).start()
        return carry

    lax.fori_loop(1, n, gk_start, 0)

    drain(parts, sum_recv)

    def add_part(at, value):
        return value + parts[at]

    gathered[span(me), :] = lax.fori_loop(0, n - 1, add_part, total[span(me), :])

    def all_start(off, carry):
        target = lax.rem(me + off, n)
        remote(
            gathered.at[span(me)], gathered.at[span(me)], all_send, all_recv, place(target)
        ).start()
        return carry

    lax.fori_loop(1, n, all_start, 0)

    drain(gk_r, gk_recv)

    def add_kernel(at, value):
        return value + gk_r[at]

    gk_o[...] = lax.fori_loop(0, n - 1, add_kernel, gk_s[...])[0:len(OFFSETS)]

    drain(gathered.at[pl.ds(0, (n - 1) * piece)], all_recv)
    gout_o[...] = gathered[0:hidden_size, :]
    gin_o[...] = gathered[hidden_size:bias_at, :]
    gb_o[...] = gathered[bias_at:bias_at + 1, :]

    drain(sbuf.at[pl.ds(0, n - 1)], row_send)
    drain(adj_s.at[pl.ds(0, n_lon - 1)], adj_send)
    drain(dep_r.at[pl.ds(0, n_lon - 1)], dep_send)
    drain(parts, sum_send)
    drain(gathered.at[pl.ds(0, (n - 1) * piece)], all_send)
    drain(gk_r, gk_send)

    @pl.when(me < n - 1)
    def _():
        up_copy.wait_send()

    @pl.when(me > 0)
    def _():
        down_copy.wait_send()

    @pl.when(lat < n_lat - 1)
    def _():
        low_copy.wait_send()

    @pl.when(lat > 0)
    def _():
        high_copy.wait_send()


def local(
    observations, owner_device, local_cell, valid_counts,
    weight_in, bias_in, weight_out, kernel_taps, cotangent,
):
    n_lat, n_lon = lax.axis_size("lat"), lax.axis_size("lon")
    n = n_lat * n_lon
    obs_rows, feat = observations.shape
    hidden_size, channels = weight_out.shape
    own_rows, cols, _ = cotangent.shape
    tile_rows, tile_cols = own_rows * n_lon, cols // n_lon
    cells = tile_rows * tile_cols
    slots = round_up(2 * obs_rows // n, 16)
    piece = round_up(-(-(hidden_size + feat + 8) // n), 8)
    taps = kernel_taps.shape[0]
    kernel_pad = round_up(taps, 8)
    scale = 1.0 / math.sqrt(obs_rows * n)
    vmem = pl.BlockSpec(memory_space=pltpu.VMEM)
    dma = pltpu.SemaphoreType.DMA
    out = pl.pallas_call(
        functools.partial(kernel, n_lat, n_lon, slots, piece, scale),
        out_shape=(
            jax.ShapeDtypeStruct(cotangent.shape, BF16),
            jax.ShapeDtypeStruct((feat, hidden_size), F32),
            jax.ShapeDtypeStruct((1, hidden_size), F32),
            jax.ShapeDtypeStruct((hidden_size, channels), F32),
            jax.ShapeDtypeStruct((taps, channels), F32),
        ),
        in_specs=[vmem, vmem, vmem, pl.BlockSpec(memory_space=pltpu.SMEM)] + [vmem] * 5,
        out_specs=(vmem,) * 5,
        scratch_shapes=[
            pltpu.VMEM((2 * n, 128), F32),
            pltpu.VMEM((1, obs_rows), jnp.int32),
            pltpu.VMEM((n, slots + META, feat), BF16),
            pltpu.VMEM((n, slots + META, feat), BF16),
            pltpu.VMEM((cols, channels), BF16),
            pltpu.VMEM((cols, channels), BF16),
            pltpu.VMEM((n_lon, own_rows, tile_cols, channels), BF16),
            pltpu.VMEM((n_lon, own_rows, tile_cols, channels), BF16),
            pltpu.VMEM((cells, channels), F32),
            pltpu.VMEM((cells, channels), BF16),
            pltpu.VMEM((cells, channels), F32),
            pltpu.VMEM((tile_rows + 2, tile_cols, channels), BF16),
            pltpu.VMEM((n_lon, own_rows + 2, tile_cols, channels), BF16),
            pltpu.VMEM((n_lon, tile_cols, channels), BF16),
            pltpu.VMEM((n_lon, tile_cols, channels), BF16),
            pltpu.VMEM((own_rows + 2, cols, channels), F32),
            pltpu.VMEM((n * piece, channels), F32),
            pltpu.VMEM((n - 1, piece, channels), F32),
            pltpu.VMEM((n * piece, channels), F32),
            pltpu.VMEM((kernel_pad, channels), F32),
            pltpu.VMEM((n - 1, kernel_pad, channels), F32),
            dma, dma((n // GROUP,)), dma((2,)), dma((2,)), dma, dma, dma, dma,
            dma((2,)), dma((2,)), dma, dma, dma, dma, dma, dma,
        ],
        compiler_params=pltpu.CompilerParams(
            collective_id=0, has_side_effects=True, vmem_limit_bytes=60 * 1024 * 1024
        ),
    )(
        observations, owner_device.reshape(1, obs_rows), local_cell.reshape(1, obs_rows),
        valid_counts, weight_in, bias_in.reshape(1, hidden_size), weight_out, kernel_taps, cotangent,
    )
    grid_out, grad_in, grad_bias, grad_out, grad_kernel = out
    return (grid_out, grad_in, grad_bias.reshape(hidden_size), grad_out, grad_kernel)


def solution(mesh):
    return jax.shard_map(
        local,
        mesh=mesh,
        in_specs=(
            P(("lat", "lon"), None),
            P(("lat", "lon"), None),
            P(("lat", "lon")),
            P(("lat", "lon")),
            P(),
            P(),
            P(),
            P(),
            P(("lat", "lon"), None, None),
        ),
        out_specs=(P(("lat", "lon"), None, None), P(), P(), P(), P()),
        check_vma=False,
    )
```

time: 272 us -> 78 us (0.29)
  the two profiles are of different devices: /device:TPU:0 before, /device:TPU:29 now
where the time goes in v1:
time: 78 us; the launch traced here: 77.7 us
  Pallas kernels  70.9 us (91%)
  local copies, waits for them, and re-layouts  5.51 us (7%)
  between operations  1.31 us (2%)
    pallas_call x1, Pallas kernels, local(): pl.pallas_call(functools.partial(kernel, n_lat, n_lon, slots, piece, scal...  70.9 us
    unnamed x13, local copies, waits for them, and re-layouts  4.22 us

profile of v1, /device:TPU:29, one launch (start us, length us, event | category | flops | bytes accessed | tf_op | source)
XLA Modules:
  0.0 77.7 jit_solution(10734042594338937285)
XLA Ops:
  1.3 1.3 %reshape.23.cell = s32[1,1536]{1,0:T(1,128)} reshape(s32[1536]{0:T(1024)} %param.11) | data formatting | bytes 12288 | tf_op jit(solution)/shard_map/reshape | solution.py:443
  2.6 70.9 %shard_map.128 = (bf16[2,192,256]{2,1,0:T(8,128)(2,1)}, f32[128,256]{1,0:T(8,128)}, f32[1,256]{1,0:T(1,128)}, f32[256,256]{1,0:T(8,128)}, f32[9,256]{1,0:T(8,128)}) custom-call(bf16[1536,128]{1,0:T(8,128)(2,1)} %obs.1, s32[1,1536]{1,0:T(1,128)} %bitcast.3, s32[1,1536]{1,0:T(1,128)} %reshape.23.cell, s32[1]{0:T(128)S(6)} %copy.19.count, ...), custom_call_target="tpu_custom_call" | custom-call | tf_op jit(solution)/shard_map/pallas_call | solution.py:403
  73.5 0.0 copy-start.1
  73.5 0.0 copy-start
  73.5 1.7 %copy.20 = bf16[2,192,256]{2,1,0:T(8,128)(2,1)} copy(bf16[2,192,256]{2,1,0:T(8,128)(2,1)} %get-tuple-element.20) | data formatting | bytes 393216
  75.1 0.0 copy-done.1
  75.1 0.0 copy-start.3
  75.1 0.7 copy.21
  75.8 0.0 copy-done.3
  75.8 0.6 copy.22
  76.4 0.0 copy-done
  76.4 0.0 copy-start.2
  76.4 0.7 copy.23
  77.1 0.0 copy-done.2
  77.1 0.6 copy.24
Async XLA Ops:
  73.5 1.7 %copy-start.1 = (f32[128,256]{1,0:T(8,128)S(1)}, f32[128,256]{1,0:T(8,128)}, u32[]{:S(2)}) copy-start(f32[128,256]{1,0:T(8,128)} %get-tuple-element.21) | copy-start | bytes 393220
  73.5 2.9 %copy-start = (f32[256,256]{1,0:T(8,128)S(1)}, f32[256,256]{1,0:T(8,128)}, u32[]{:S(2)}) copy-start(f32[256,256]{1,0:T(8,128)} %get-tuple-element.23) | copy-start | bytes 786436
  75.1 0.7 copy-start.3
  76.4 0.7 copy-start.2

commit v2 on v1

--- a/solution.py
+++ b/solution.py
@@ -34,7 +34,7 @@
     obs, owner, cell, count, w_in, b_in, w_out, taps, cot,
     grid_o, gin_o, gb_o, gout_o, gk_o,
     meta, slot_row, sbuf, rbuf, cot_top, cot_bot, adj_s, adj_r, adj_f, adj_b,
-    dep, dep_b, dep_r, hal_top, hal_bot, strip, total, parts, gathered, gk_s, gk_r,
+    dep, dep_b, dep_r, hal_top, hal_bot, strip, total, rounded, parts, gathered, gk_s, gk_lon, gk_lat,
     row_send, row_recv, cot_send, cot_recv, adj_send, adj_recv, dep_send, dep_recv,
     hal_send, hal_recv, sum_send, sum_recv, all_send, all_recv, gk_send, gk_recv,
 ):
@@ -48,9 +48,17 @@
     cells = tile_rows * tile_cols
     hidden_size = w_in.shape[1]
     groups = n // GROUP
+    used = -(-(hidden_size + feat + 16) // piece)
 
     def place(target):
         return (target // n_lon, lax.rem(target, n_lon))
+
+    def partner(turn):
+        return (lax.rem(lat + lax.rem(turn, n_lat), n_lat), lax.rem(lon + turn // n_lat, n_lon))
+
+    def number(turn):
+        to_lat, to_lon = partner(turn)
+        return to_lat * n_lon + to_lon
 
     def remote(src, dst, send, recv, device):
         return pltpu.make_async_remote_copy(
@@ -131,21 +139,21 @@
 
     def row_copy(off, g):
         return remote(
-            sbuf.at[off], rbuf.at[off], row_send, row_recv.at[g], place(lax.rem(me + off, n))
+            sbuf.at[off], rbuf.at[off], row_send, row_recv.at[g], partner(off)
         )
 
     def send_group(g, carry, first=False):
         ids = slot_row[...]
         picks = []
         for q in range(GROUP):
-            target = lax.rem(me + g * GROUP + q, n)
+            target = number(g * GROUP + q)
             pick = (ids - target * slots) == iota((slots, obs_rows), 0)
             picks.append(pick.astype(F32).astype(BF16))
         rows = dot(jnp.concatenate(picks, axis=0), obs[...]).astype(BF16)
         line = iota((META, 128), 0)
         for q in range(GROUP):
             off = g * GROUP + q
-            target = lax.rem(me + off, n)
+            target = number(off)
             sbuf[off, :slots, :] = rows[q * slots:(q + 1) * slots]
             tail = jnp.where(
                 line == 0, meta[pl.ds(target, 1), :],
@@ -277,13 +285,20 @@
     dep_r[lon] = dep_b[pl.ds(lon * own_rows, own_rows + 2)]
 
     def span(at):
-        return pl.ds(pl.multiple_of(at * piece, 8), piece)
+        return pl.ds(pl.multiple_of(at * piece, 16), piece)
 
     def sum_start(off, carry):
-        target = lax.rem(me + off, n)
-        remote(total.at[span(target)], parts.at[off - 1], sum_send, sum_recv, place(target)).start()
+        target = number(off)
+
+        @pl.when(target < used)
+        def _():
+            remote(
+                rounded.at[span(target)], parts.at[off - 1], sum_send, sum_recv, partner(off)
+            ).start()
+
         return carry
 
+    rounded[...] = total[...].astype(BF16)
     lax.fori_loop(1, n, sum_start, 0)
 
     drain(dep_r.at[pl.ds(0, n_lon - 1)], dep_recv)
@@ -320,50 +335,78 @@
                     )
     for y in range(own_rows):
         grid_o[y] = fields[y].astype(BF16)
-    spare = gk_s.shape[0] - len(OFFSETS)
-    gk_s[...] = scale * jnp.concatenate(kernel_rows + [jnp.zeros((spare, channels), F32)], axis=0)
-
-    def gk_start(off, carry):
-        target = lax.rem(me + off, n)
-        remote(gk_s, gk_r.at[off - 1], gk_send, gk_recv, place(target)).start()
-        return carry
-
-    lax.fori_loop(1, n, gk_start, 0)
-
-    drain(parts, sum_recv)
-
-    def add_part(at, value):
-        return value + parts[at]
-
-    gathered[span(me), :] = lax.fori_loop(0, n - 1, add_part, total[span(me), :])
-
-    def all_start(off, carry):
-        target = lax.rem(me + off, n)
+    spare = gk_s.shape[1] - len(OFFSETS)
+    grad_taps = scale * jnp.concatenate(kernel_rows + [jnp.zeros((spare, channels), F32)], axis=0)
+    gk_s[0] = grad_taps.astype(BF16)
+    for step in range(1, n_lon):
         remote(
-            gathered.at[span(me)], gathered.at[span(me)], all_send, all_recv, place(target)
+            gk_s.at[0], gk_lon.at[lon], gk_send.at[0], gk_recv.at[0],
+            (lat, lax.rem(lon + step, n_lon)),
         ).start()
-        return carry
-
-    lax.fori_loop(1, n, all_start, 0)
-
-    drain(gk_r, gk_recv)
-
-    def add_kernel(at, value):
-        return value + gk_r[at]
-
-    gk_o[...] = lax.fori_loop(0, n - 1, add_kernel, gk_s[...])[0:len(OFFSETS)]
-
-    drain(gathered.at[pl.ds(0, (n - 1) * piece)], all_recv)
-    gout_o[...] = gathered[0:hidden_size, :]
-    gin_o[...] = gathered[hidden_size:bias_at, :]
-    gb_o[...] = gathered[bias_at:bias_at + 1, :]
+
+    @pl.when(me < used)
+    def _():
+        drain(parts, sum_recv)
+
+        def add_part(at, value):
+            return value + parts[at].astype(F32)
+
+        gathered[span(me), :] = lax.fori_loop(
+            0, n - 1, add_part, total[span(me), :]
+        ).astype(BF16)
+
+        def all_start(off, carry):
+            remote(
+                gathered.at[span(me)], gathered.at[span(me)], all_send, all_recv, partner(off)
+            ).start()
+            return carry
+
+        lax.fori_loop(1, n, all_start, 0)
+
+    gk_lon[lon] = gk_s[0]
+    drain(gk_lon.at[pl.ds(0, n_lon - 1)], gk_recv.at[0])
+    grad_taps = gk_lon[0].astype(F32)
+    for at in range(1, n_lon):
+        grad_taps = grad_taps + gk_lon[at].astype(F32)
+    gk_s[1] = grad_taps.astype(BF16)
+    for step in range(1, n_lat):
+        remote(
+            gk_s.at[1], gk_lat.at[lat], gk_send.at[1], gk_recv.at[1],
+            (lax.rem(lat + step, n_lat), lon),
+        ).start()
+    gk_lat[lat] = gk_s[1]
+    drain(gk_lat.at[pl.ds(0, n_lat - 1)], gk_recv.at[1])
+    grad_taps = gk_lat[0].astype(F32)
+    for at in range(1, n_lat):
+        grad_taps = grad_taps + gk_lat[at].astype(F32)
+    gk_o[...] = grad_taps[0:len(OFFSETS)]
+
+    @pl.when(me < used)
+    def _():
+        drain(gathered.at[pl.ds(0, (used - 1) * piece)], all_recv)
+
+    @pl.when(me >= used)
+    def _():
+        drain(gathered.at[pl.ds(0, used * piece)], all_recv)
+
+    gout_o[...] = gathered[0:hidden_size, :].astype(F32)
+    gin_o[...] = gathered[hidden_size:bias_at, :].astype(F32)
+    gb_o[...] = gathered[bias_at:bias_at + 16, :].astype(F32)[0:1]
 
     drain(sbuf.at[pl.ds(0, n - 1)], row_send)
     drain(adj_s.at[pl.ds(0, n_lon - 1)], adj_send)
     drain(dep_r.at[pl.ds(0, n_lon - 1)], dep_send)
-    drain(parts, sum_send)
-    drain(gathered.at[pl.ds(0, (n - 1) * piece)], all_send)
-    drain(gk_r, gk_send)
+    drain(gk_lon.at[pl.ds(0, n_lon - 1)], gk_send.at[0])
+    drain(gk_lat.at[pl.ds(0, n_lat - 1)], gk_send.at[1])
+
+    @pl.when(me < used)
+    def _():
+        drain(gathered.at[pl.ds(0, (used - 1) * piece)], sum_send)
+        drain(gathered.at[pl.ds(0, (n - 1) * piece)], all_send)
+
+    @pl.when(me >= used)
+    def _():
+        drain(gathered.at[pl.ds(0, used * piece)], sum_send)
 
     @pl.when(me < n - 1)
     def _():
@@ -394,9 +437,9 @@
     tile_rows, tile_cols = own_rows * n_lon, cols // n_lon
     cells = tile_rows * tile_cols
     slots = round_up(2 * obs_rows // n, 16)
-    piece = round_up(-(-(hidden_size + feat + 8) // n), 8)
+    piece = round_up(-(-(hidden_size + feat + 16) // n), 16)
     taps = kernel_taps.shape[0]
-    kernel_pad = round_up(taps, 8)
+    kernel_pad = round_up(taps, 16)
     scale = 1.0 / math.sqrt(obs_rows * n)
     vmem = pl.BlockSpec(memory_space=pltpu.VMEM)
     dma = pltpu.SemaphoreType.DMA
@@ -429,12 +472,14 @@
             pltpu.VMEM((n_lon, tile_cols, channels), BF16),
             pltpu.VMEM((own_rows + 2, cols, channels), F32),
             pltpu.VMEM((n * piece, channels), F32),
-            pltpu.VMEM((n - 1, piece, channels), F32),
-            pltpu.VMEM((n * piece, channels), F32),
-            pltpu.VMEM((kernel_pad, channels), F32),
-            pltpu.VMEM((n - 1, kernel_pad, channels), F32),
+            pltpu.VMEM((n * piece, channels), BF16),
+            pltpu.VMEM((n - 1, piece, channels), BF16),
+            pltpu.VMEM((n * piece, channels), BF16),
+            pltpu.VMEM((2, kernel_pad, channels), BF16),
+            pltpu.VMEM((n_lon, kernel_pad, channels), BF16),
+            pltpu.VMEM((n_lat, kernel_pad, channels), BF16),
             dma, dma((n // GROUP,)), dma((2,)), dma((2,)), dma, dma, dma, dma,
-            dma((2,)), dma((2,)), dma, dma, dma, dma, dma, dma,
+            dma((2,)), dma((2,)), dma, dma, dma, dma, dma((2,)), dma((2,)),
         ],
         compiler_params=pltpu.CompilerParams(
             collective_id=0, has_side_effects=True, vmem_limit_bytes=60 * 1024 * 1024

time: 78 us -> 58 us (0.74)
  the two profiles are of different devices: /device:TPU:29 before, /device:TPU:0 now
where the time goes in v2:
time: 58 us; the launch traced here: 57.6 us
  Pallas kernels  50.8 us (88%)
  local copies, waits for them, and re-layouts  5.51 us (10%)
  between operations  1.31 us (2%)
    pallas_call x1, Pallas kernels, local(): pl.pallas_call(functools.partial(kernel, n_lat, n_lon, slots, piece, scal...  50.8 us
    unnamed x13, local copies, waits for them, and re-layouts  4.22 us
    reshape x1, local copies, waits for them, and re-layouts, local(): local_cell.reshape(1, obs_rows)  1.3 us

profile of v2, /device:TPU:0, one launch (start us, length us, event | category | flops | bytes accessed | tf_op | source)
XLA Modules:
  0.0 57.6 jit_solution(13351830203162231785)
XLA Ops:
  1.3 1.3 %reshape.23.cell = s32[1,1536]{1,0:T(1,128)} reshape(s32[1536]{0:T(1024)} %param.11) | data formatting | bytes 12288 | tf_op jit(solution)/shard_map/reshape | solution.py:488
  2.6 50.8 %shard_map.128 = (bf16[2,192,256]{2,1,0:T(8,128)(2,1)}, f32[128,256]{1,0:T(8,128)}, f32[1,256]{1,0:T(1,128)}, f32[256,256]{1,0:T(8,128)}, f32[9,256]{1,0:T(8,128)}) custom-call(bf16[1536,128]{1,0:T(8,128)(2,1)} %obs.1, s32[1,1536]{1,0:T(1,128)} %bitcast.3, s32[1,1536]{1,0:T(1,128)} %reshape.23.cell, s32[1]{0:T(128)S(6)} %copy.19.count, ...), custom_call_target="tpu_custom_call" | custom-call | tf_op jit(solution)/shard_map/pallas_call | solution.py:446
  53.4 0.0 copy-start.1
  53.4 0.0 copy-start
  53.4 1.7 %copy.20 = bf16[2,192,256]{2,1,0:T(8,128)(2,1)} copy(bf16[2,192,256]{2,1,0:T(8,128)(2,1)} %get-tuple-element.20) | data formatting | bytes 393216
  55.1 0.0 copy-done.1
  55.1 0.0 copy-start.3
  55.1 0.7 %copy.21 = f32[128,256]{1,0:T(8,128)} copy(f32[128,256]{1,0:T(8,128)S(1)} %copy-done.1) | data formatting | bytes 262144
  55.7 0.0 copy-done.3
  55.7 0.6 copy.22
  56.3 0.0 copy-done
  56.3 0.0 copy-start.2
  56.3 0.7 %copy.23 = f32[256,256]{1,0:T(8,128)} copy(f32[256,256]{1,0:T(8,128)S(1)} %copy-done) | data formatting | bytes 524288
  57.0 0.0 copy-done.2
  57.0 0.6 %copy.24 = f32[9,256]{1,0:T(8,128)} copy(f32[9,256]{1,0:T(8,128)S(1)} %copy-done.2) | data formatting | bytes 18432
Async XLA Ops:
  53.4 1.7 %copy-start.1 = (f32[128,256]{1,0:T(8,128)S(1)}, f32[128,256]{1,0:T(8,128)}, u32[]{:S(2)}) copy-start(f32[128,256]{1,0:T(8,128)} %get-tuple-element.21) | copy-start | bytes 393220
  53.4 2.9 %copy-start = (f32[256,256]{1,0:T(8,128)S(1)}, f32[256,256]{1,0:T(8,128)}, u32[]{:S(2)}) copy-start(f32[256,256]{1,0:T(8,128)} %get-tuple-element.23) | copy-start | bytes 786436
  55.1 0.7 %copy-start.3 = (f32[1,256]{1,0:T(1,128)S(1)}, f32[1,256]{1,0:T(1,128)}, u32[]{:S(2)}) copy-start(f32[1,256]{1,0:T(1,128)} %get-tuple-element.12) | copy-start | bytes 3076
  56.3 0.7 %copy-start.2 = (f32[9,256]{1,0:T(8,128)S(1)}, f32[9,256]{1,0:T(8,128)}, u32[]{:S(2)}) copy-start(f32[9,256]{1,0:T(8,128)} %get-tuple-element.24) | copy-start | bytes 27652

commit v3 on v2

--- a/solution.py
+++ b/solution.py
@@ -168,6 +168,7 @@
         return carry
 
     send_group(0, 0, True)
+    lax.fori_loop(1, groups, send_group, 0)
 
     @pl.when(me > 0)
     def _():
@@ -206,8 +207,6 @@
     for step in range(1, n_lon):
         adj_copy(step).start()
     adj_r[lon] = adj_s[lon]
-
-    lax.fori_loop(1, groups, send_group, 0)
 
     drain(adj_r.at[pl.ds(0, n_lon - 1)], adj_recv)
     for k in range(n_lon):

time: 58 us -> 56.6 us (0.976)
  Pallas kernels: 50.8 us -> 49.4 us
    pallas_call x1, Pallas kernels: 50.8 us -> 49.4 us  [local(): pl.pallas_call(functools.partial(kernel, n_lat, n_lon, slots, piece, scal...]
where the time goes in v3:
time: 56.6 us; the launch traced here: 56.2 us
  Pallas kernels  49.4 us (87%)
  local copies, waits for them, and re-layouts  5.51 us (10%)
  between operations  1.31 us (2%)
    pallas_call x1, Pallas kernels, local(): pl.pallas_call(functools.partial(kernel, n_lat, n_lon, slots, piece, scal...  49.4 us
    unnamed x13, local copies, waits for them, and re-layouts  4.22 us
    reshape x1, local copies, waits for them, and re-layouts, local(): local_cell.reshape(1, obs_rows)  1.3 us

profile of v3, /device:TPU:0, one launch (start us, length us, event | category | flops | bytes accessed | tf_op | source)
XLA Modules:
  0.0 56.2 jit_solution(4822926630827351619)
XLA Ops:
  1.3 1.3 %reshape.23.cell = s32[1,1536]{1,0:T(1,128)} reshape(s32[1536]{0:T(1024)} %param.11) | data formatting | bytes 12288 | tf_op jit(solution)/shard_map/reshape | solution.py:487
  2.6 49.4 %shard_map.128 = (bf16[2,192,256]{2,1,0:T(8,128)(2,1)}, f32[128,256]{1,0:T(8,128)}, f32[1,256]{1,0:T(1,128)}, f32[256,256]{1,0:T(8,128)}, f32[9,256]{1,0:T(8,128)}) custom-call(bf16[1536,128]{1,0:T(8,128)(2,1)} %obs.1, s32[1,1536]{1,0:T(1,128)} %bitcast.3, s32[1,1536]{1,0:T(1,128)} %reshape.23.cell, s32[1]{0:T(128)S(6)} %copy.19.count, ...), custom_call_target="tpu_custom_call" | custom-call | tf_op jit(solution)/shard_map/pallas_call | solution.py:445
  52.0 0.0 copy-start.1
  52.0 0.0 copy-start
  52.0 1.7 %copy.20 = bf16[2,192,256]{2,1,0:T(8,128)(2,1)} copy(bf16[2,192,256]{2,1,0:T(8,128)(2,1)} %get-tuple-element.20) | data formatting | bytes 393216
  53.7 0.0 copy-done.1
  53.7 0.0 copy-start.3
  53.7 0.7 %copy.21 = f32[128,256]{1,0:T(8,128)} copy(f32[128,256]{1,0:T(8,128)S(1)} %copy-done.1) | data formatting | bytes 262144
  54.3 0.0 copy-done.3
  54.3 0.6 %copy.22 = f32[256]{0:T(256)} copy(f32[256]{0:T(256)S(1)} %bitcast.5) | data formatting | bytes 2048
  54.9 0.0 copy-done
  54.9 0.0 copy-start.2
  54.9 0.7 %copy.23 = f32[256,256]{1,0:T(8,128)} copy(f32[256,256]{1,0:T(8,128)S(1)} %copy-done) | data formatting | bytes 524288
  55.6 0.0 copy-done.2
  55.6 0.6 %copy.24 = f32[9,256]{1,0:T(8,128)} copy(f32[9,256]{1,0:T(8,128)S(1)} %copy-done.2) | data formatting | bytes 18432
Async XLA Ops:
  52.0 1.7 %copy-start.1 = (f32[128,256]{1,0:T(8,128)S(1)}, f32[128,256]{1,0:T(8,128)}, u32[]{:S(2)}) copy-start(f32[128,256]{1,0:T(8,128)} %get-tuple-element.21) | copy-start | bytes 393220
  52.0 2.9 %copy-start = (f32[256,256]{1,0:T(8,128)S(1)}, f32[256,256]{1,0:T(8,128)}, u32[]{:S(2)}) copy-start(f32[256,256]{1,0:T(8,128)} %get-tuple-element.23) | copy-start | bytes 786436
  53.7 0.7 %copy-start.3 = (f32[1,256]{1,0:T(1,128)S(1)}, f32[1,256]{1,0:T(1,128)}, u32[]{:S(2)}) copy-start(f32[1,256]{1,0:T(1,128)} %get-tuple-element.12) | copy-start | bytes 3076
  54.9 0.7 %copy-start.2 = (f32[9,256]{1,0:T(8,128)S(1)}, f32[9,256]{1,0:T(8,128)}, u32[]{:S(2)}) copy-start(f32[9,256]{1,0:T(8,128)} %get-tuple-element.24) | copy-start | bytes 27652
